TPU v7x, 128 devices: a whole 4x4x4 slice. The times are simulated.
128 devices in a mesh: gx: 4 (over y_hi, core), gy: 8 (over y_lo, z), gz: 4 (over x).
Axes of the slice: x: 4, y: 4 (y_hi: 2, y_lo: 2; y = y_hi * 2 + y_lo), z: 4, core: 2. Of those that a mesh axis runs over, the one named last changes fastest.
Arguments:
- start_field: float32 [256, 512, 1024], P('gx', 'gy', 'gz'), may hold values from -6 to 6
- right_side: float32 [256, 512, 1024], P('gx', 'gy', 'gz'), may hold values from -6 to 6
Outputs:
- corrected: float32 [256, 512, 1024], P('gx', 'gy', 'gz')
All inputs are finite; a program needn't handle non-finite values.
Results may differ from a plain program's by a relative error of at most 0.00002.
Values sent between devices are 32-bit elements; how exact they have to be, the bound alone decides.
A program may use at most 128 MiB of HBM per device.

v0:
```python
import functools

import jax
import jax.numpy as jnp
from jax import lax
from jax.experimental import pallas as pl
from jax.experimental.pallas import tpu as pltpu
from jax.sharding import PartitionSpec as P

MESH = pl.DeviceIdType.MESH
F32 = jnp.float32
BF16 = jnp.bfloat16
SEVENTH = 1.0 / 7.0
AXES = ("gx", "gy", "gz")
SEND = {-1: (3, 4), 0: (3, 34), 1: (32, 5)}
LAND = {-1: 35, 0: 3, 1: 0}
TSEND = {-1: (0, 1), 0: (0, 3), 1: (2, 1)}
TLAND = {-1: 2, 0: 0, 1: 0}
XY = [(dx, dy) for dx in (-1, 0, 1) for dy in (-1, 0, 1)]
XY8 = [d for d in XY if d != (0, 0)]


def split3(v):
    hi = v.astype(BF16)
    rest = v - hi.astype(F32)
    mid = rest.astype(BF16)
    lo = (rest - mid.astype(F32)).astype(BF16)
    return hi, mid, lo


def dot3(v, weights):
    parts = [jnp.dot(p, weights, preferred_element_type=F32) for p in split3(v)]
    return (parts[2] + parts[1]) + parts[0]


def kernel(s_in, b_in, out, *scratch):
    (u0, u1, u2, bv, ez, zr, at, qb, wr, wp, gm, gs, lh, ls, kc, g2, ca, cb, fz, wt) = scratch[:20]
    rm = scratch[20:28]
    rl = scratch[28:36]
    rz = scratch[36:45]
    load_sem, out_sem, f_send, f_recv, m_send, m_recv, l_send, l_recv, z_send, z_recv = scratch[45:]

    gx, gy, gz = (lax.axis_index(a) for a in AXES)
    nx, ny, nz = (lax.axis_size(a) for a in AXES)
    me = {"gx": gx, "gy": gy, "gz": gz}
    size = {"gx": nx, "gy": ny, "gz": nz}

    def has(axis, d):
        if d == 0:
            return True
        return me[axis] < size[axis] - 1 if d > 0 else me[axis] > 0

    def has_all(dx, dy, dz):
        ok = None
        for axis, d in zip(AXES, (dx, dy, dz)):
            if d:
                here = has(axis, d)
                ok = here if ok is None else jnp.logical_and(ok, here)
        return ok

    def target(dx, dy, dz):
        return {a: me[a] + d for a, d in zip(AXES, (dx, dy, dz))}

    loads = []
    for h in range(2):
        lanes = pl.ds(128 * h, 128)
        loads.append(pltpu.make_async_copy(s_in.at[:, :, lanes], u0.at[pl.ds(1, 64), h, pl.ds(8, 64), :], load_sem.at[h]))
    for h in range(2):
        lanes = pl.ds(128 * h, 128)
        loads.append(pltpu.make_async_copy(b_in.at[:, :, lanes], bv.at[pl.ds(2, 64), h], load_sem.at[2 + h]))
    for c in loads:
        c.start()

    barrier = pltpu.get_barrier_semaphore()
    count = jnp.int32(0)
    for axis in AXES:
        for d in (-1, 1):
            ok = has(axis, d)
            count = count + ok.astype(jnp.int32)

            @pl.when(ok)
            def _():
                pl.semaphore_signal(barrier, inc=1, device_id={axis: me[axis] + d}, device_id_type=MESH)

    lane = lax.broadcasted_iota(jnp.int32, (64, 128), 1)
    first = lane == 0
    last = lane == 127
    group = lax.rem((lane + 1) // 2, 64)

    zplane = jnp.zeros((2, 80, 128), F32)
    zrow = jnp.zeros((1, 128), F32)

    @pl.when(gx == 0)
    def _():
        u0[0] = zplane
        u1[0] = zplane

    @pl.when(gx == nx - 1)
    def _():
        u0[65] = zplane
        u1[65] = zplane

    def zero_rows(row):
        def body(x, _):
            for h in range(2):
                u0[x, h, pl.ds(row, 1), :] = zrow
                u1[x, h, pl.ds(row, 1), :] = zrow
            return 0

        lax.fori_loop(1, 65, body, 0)

    @pl.when(gy == 0)
    def _():
        zero_rows(7)

    @pl.when(gy == ny - 1)
    def _():
        zero_rows(72)

    @pl.when(gz == 0)
    def _():
        zr[0, 0] = jnp.zeros((64, 128), F32)
        zr[1, 0] = jnp.zeros((64, 128), F32)

    @pl.when(gz == nz - 1)
    def _():
        zr[0, 1] = jnp.zeros((64, 128), F32)
        zr[1, 1] = jnp.zeros((64, 128), F32)

    for p in (0, 1, 2, 67, 68, 69, 70):
        u2[p] = zplane
    for p in (0, 1, 66, 67, 68):
        bv[p] = jnp.zeros((2, 64, 128), F32)
    at[...] = jnp.zeros(at.shape, F32)

    def coarse_of(column):
        inner = column - 128
        return jnp.where(column < 128, column, jnp.where(inner >= 64, inner - 128, inner + 128))

    zi = lax.broadcasted_iota(jnp.int32, (256, 256), 0)
    kci = coarse_of(lax.broadcasted_iota(jnp.int32, (256, 256), 1))
    d = zi - 2 * kci
    zero = jnp.zeros((256, 256), F32)
    plain = jnp.where(d == 1, -2.0, jnp.where((d == 0) | (d == 2), -1.0, zero))
    topz = (gz == nz - 1).astype(F32)
    edge = jnp.where((zi == 255) & (kci == 127), topz, zero)
    around = jnp.where((d >= 0) & (d <= 2), 2.0, jnp.where((d == -1) | (d == 3), 1.0, zero)) - edge
    wr[pl.ds(0, 256), :] = plain.astype(BF16)
    wr[pl.ds(256, 256), :] = around.astype(BF16)
    kr = coarse_of(lax.broadcasted_iota(jnp.int32, (256, 256), 0))
    d = lax.broadcasted_iota(jnp.int32, (256, 256), 1) - 2 * kr
    wp[...] = jnp.where(d == 1, 1.0, jnp.where((d == 0) | (d == 2), 0.5, zero)).astype(BF16)

    r40 = lax.broadcasted_iota(jnp.int32, (40, 128), 0)
    l40 = lax.broadcasted_iota(jnp.int32, (40, 128), 1)
    zero40 = jnp.zeros((40, 128), F32)
    low_y = jnp.where(gy > 0, 0, 4)
    high_y = jnp.where(gy < ny - 1, 40, 36)
    low_z = jnp.where(gz > 0, 124, 128)
    high_z = jnp.where(gz < nz - 1, 4, 0)
    rows_in = jnp.where((r40 >= low_y) & (r40 < high_y), SEVENTH, zero40)
    kc[0] = rows_in
    kc[1] = jnp.where((l40 >= low_z) | (l40 < high_z), rows_in, zero40)
    topy = (gy == ny - 1).astype(F32)
    kc[2] = 0.5 - jnp.where(r40 == 35, 0.25 * topy, zero40)

    def faces(r, u):
        x_in = (slice(None), pl.ds(8, 64), slice(None))
        xs = pl.ds(1, 64)
        every = slice(None)
        plan = [
            ("gx", 1, u.at[(64,) + x_in], u.at[(0,) + x_in]),
            ("gx", -1, u.at[(1,) + x_in], u.at[(65,) + x_in]),
            ("gy", 1, u.at[xs, every, pl.ds(71, 1), every], u.at[xs, every, pl.ds(7, 1), every]),
            ("gy", -1, u.at[xs, every, pl.ds(8, 1), every], u.at[xs, every, pl.ds(72, 1), every]),
            ("gz", 1, ez.at[r], zr.at[r, 0]),
            ("gz", -1, ez.at[r], zr.at[r, 1]),
        ]
        done = []
        for k, (axis, dd, src, dst) in enumerate(plan):
            copy = pltpu.make_async_remote_copy(
                src_ref=src, dst_ref=dst, send_sem=f_send.at[r, k], recv_sem=f_recv.at[r, k],
                device_id={axis: me[axis] + dd}, device_id_type=MESH,
            )
            done.append((axis, dd, copy))
        return done

    def start(copies):
        for axis, dd, copy in copies:
            pl.when(has(axis, dd))(copy.start)

    def arrive(copies):
        for axis, dd, copy in copies:
            pl.when(has(axis, -dd))(copy.wait_recv)

    def sent(copies):
        for axis, dd, copy in copies:
            pl.when(has(axis, dd))(copy.wait_send)

    round0, round1 = faces(0, u0), faces(1, u1)

    loads[0].wait()
    loads[1].wait()
    pl.semaphore_wait(barrier, count)
    start(round0[:4])

    def pack_face(low, high, x, packed):
        both = jnp.where(first, low, high)
        return jnp.where(group == x, pltpu.roll(both, 2 * x, 1), packed)

    def pack(x, packed):
        return pack_face(u0[x + 1, 0, pl.ds(8, 64), :], u0[x + 1, 1, pl.ds(8, 64), :], x, packed)

    ez[0] = lax.fori_loop(0, 64, pack, jnp.zeros((64, 128), F32), unroll=4)
    start(round0[4:])

    def sweep(r, u, off, v, voff):
        even = lax.rem(lane, 2) == 0
        halo = jnp.where(even, pltpu.roll(zr[r, 0], 1, 1), pltpu.roll(zr[r, 1], 127, 1))
        zr[r, 0] = halo

        def body(x, packed):
            side = pltpu.roll(zr[r, 0], lax.rem(128 - 2 * x, 128), 1)
            c = [u[x + off, h, pl.ds(8, 64), :] for h in range(2)]
            right = [pltpu.roll(c[h], 1, 1) for h in range(2)]
            left = [pltpu.roll(c[h], 127, 1) for h in range(2)]
            below = [jnp.where(first, side, right[0]), jnp.where(first, right[0], right[1])]
            above = [jnp.where(last, left[1], left[0]), jnp.where(last, side, left[1])]
            new = []
            for h in range(2):
                total = u[x + off - 1, h, pl.ds(8, 64), :] + u[x + off + 1, h, pl.ds(8, 64), :]
                total = total + (u[x + off, h, pl.ds(7, 64), :] + u[x + off, h, pl.ds(9, 64), :])
                total = total + (c[h] + bv[x + 2, h])
                total = (total + (below[h] + above[h])) * SEVENTH
                v[x + voff, h, pl.ds(8, 64), :] = total
                new.append(total)
            if r == 0:
                packed = pack_face(new[0], new[1], x, packed)
            return packed

        init = jnp.zeros((64, 128), F32) if r == 0 else jnp.int32(0)
        return lax.fori_loop(0, 64, body, init, unroll=2)

    loads[2].wait()
    loads[3].wait()
    arrive(round0)
    ez[1] = sweep(0, u0, 1, u1, 1)
    start(round1)
    arrive(round1)
    sweep(1, u1, 1, u2, 3)

    topx = gx == nx - 1

    def restrict(i, _):
        slot = lax.rem(i, 2)
        mid = jnp.where(jnp.logical_and(topx, i == 32), 2.75, 2.5).astype(F32)
        for h in range(2):
            w = [u2[2 * i + k, h, pl.ds(8, 64), :] for k in range(5)]
            b = [bv[2 * i + k, h] for k in range(3)]
            beside = w[1] + w[3]
            at[slot, h, pl.ds(16, 64), :] = 0.25 * beside + 0.5 * w[2]
            load = 0.25 * (b[0] + b[2]) + 0.5 * b[1]
            at[slot, 2 + h, pl.ds(16, 64), :] = (beside - 0.25 * (w[0] + w[4])) + (mid * w[2] - load)
        for h in range(2):
            a1 = [at[slot, h, pl.ds(8 + o, 40, stride=2), :] for o in (-1, 0, 1, 2, 3)]
            a2 = [at[slot, 2 + h, pl.ds(8 + o, 40, stride=2), :] for o in (0, 1, 2)]
            beside = a1[1] + a1[3]
            main = 0.25 * (a2[0] + a2[2]) + 0.5 * a2[1]
            main = main - (0.25 * (a1[0] + a1[4]) + 0.5 * beside) - kc[2] * a1[2]
            qb[i, :, pl.ds(128 * h, 128)] = main
            qb[i, :, pl.ds(256 + 128 * h, 128)] = 0.25 * beside + 0.5 * a1[2]
        return 0

    lax.fori_loop(0, 34, restrict, 0, unroll=2)

    gm[...] = jnp.zeros(gm.shape, F32)
    gs[...] = jnp.zeros(gs.shape, F32)

    def restrict_z(n, _):
        i = 17 * n
        got = dot3(qb[pl.ds(i, 17)].reshape(680, 512), wr[...])
        main = got[:, :128].reshape(17, 40, 128)
        gm[pl.ds(i + 3, 17)] = main
        gs[pl.ds(i + 3, 17)] = main
        g2[pl.ds(i + 3, 17), 1] = got[:, 128:].reshape(17, 40, 128)
        return 0

    lax.fori_loop(0, 2, restrict_z, 0)

    edge40 = l40 >= 124
    oct40 = l40 // 8
    for t, (lo, hi) in enumerate(((3, 16), (16, 32), (32, 37))):

        def pack_ends(p, ends):
            main, halo = gm[p], g2[p, 1]
            q = p - 16 * t
            shift = lax.rem(8 * q + 4, 128)
            here = oct40 == q
            return (
                jnp.where(here, pltpu.roll(jnp.where(edge40, halo, main), shift, 1), ends[0]),
                jnp.where(here, pltpu.roll(jnp.where(edge40, main, halo), shift, 1), ends[1]),
            )

        ends = lax.fori_loop(lo, hi, pack_ends, (zero40, zero40))
        for k in range(2):
            lh[k, t] = ends[k]
            ls[k, t] = ends[k]

    messages = []
    for n, (dx, dy) in enumerate(XY8):
        (xa, xn), (ya, yn) = SEND[dx], SEND[dy]
        (ta, tn) = TSEND[dx]
        to = target(dx, dy, 0)
        messages.append((dx, dy, 0, pltpu.make_async_remote_copy(
            src_ref=gm.at[pl.ds(xa, xn), pl.ds(ya, yn), :], dst_ref=rm[n],
            send_sem=m_send.at[n], recv_sem=m_recv.at[n], device_id=to, device_id_type=MESH)))
        messages.append((dx, dy, 0, pltpu.make_async_remote_copy(
            src_ref=lh.at[:, pl.ds(ta, tn), pl.ds(ya, yn), :], dst_ref=rl[n],
            send_sem=l_send.at[n], recv_sem=l_recv.at[n], device_id=to, device_id_type=MESH)))
    for n, (dx, dy) in enumerate(XY):
        ya, yn = SEND[dy]
        ta, tn = TSEND[dx]
        for dz in (-1, 1):
            end = 1 if dz > 0 else 0
            messages.append((dx, dy, dz, pltpu.make_async_remote_copy(
                src_ref=lh.at[end, pl.ds(ta, tn), pl.ds(ya, yn), :], dst_ref=rz[n].at[1 - end],
                send_sem=z_send.at[n, end], recv_sem=z_recv.at[n, end],
                device_id=target(dx, dy, dz), device_id_type=MESH)))
    for dx, dy, dz, copy in messages:
        pl.when(has_all(dx, dy, dz))(copy.start)

    for n, (dx, dy, dz, copy) in enumerate(messages):
        xn, yn, tn = SEND[dx][1], SEND[dy][1], TSEND[dx][1]
        xl, yl, tl = LAND[dx], LAND[dy], TLAND[dx]

        @pl.when(has_all(-dx, -dy, -dz))
        def _():
            copy.wait_recv()
            rows = pl.ds(yl, yn)
            if dz == 0 and n % 2 == 0:
                src = rm[n // 2]

                def add(p, _):
                    gs[xl + p, rows, :] = gs[xl + p, rows, :] + src[p]
                    return 0

                lax.fori_loop(0, xn, add, 0)
            elif dz == 0:
                src = rl[n // 2]
                for k in range(2):
                    for t in range(tn):
                        ls[k, tl + t, rows, :] = ls[k, tl + t, rows, :] + src[k, t]
            else:
                k = 0 if dz > 0 else 1
                src = rz[(n - 16) // 2]
                for t in range(tn):
                    ls[k, tl + t, rows, :] = ls[k, tl + t, rows, :] + src[k, t]

    begin40 = l40 < 4
    zpad = jnp.zeros((40, 2, 8, 128), F32)
    for c in (ca, cb):
        c[:, :, pl.ds(0, 8), :] = zpad
        c[:, :, pl.ds(48, 8), :] = zpad

    def assemble(p, _):
        t = p // 16
        q = p - 16 * t
        shift = lax.rem(252 - 8 * q, 128)
        low = pltpu.roll(ls[0, t], shift, 1)
        high = pltpu.roll(ls[1, t], shift, 1)
        main = jnp.where(begin40, low, jnp.where(edge40, high, gs[p]))
        halo = jnp.where(begin40, high, jnp.where(edge40, low, zero40))
        g2[p, 0] = main
        g2[p, 1] = halo
        ca[p, 0, pl.ds(8, 40), :] = main * kc[0]
        ca[p, 1, pl.ds(8, 40), :] = halo * kc[1]
        return 0

    lax.fori_loop(0, 40, assemble, 0, unroll=2)

    zc = jnp.zeros((2, 40, 128), F32)

    def clip(c):
        @pl.when(gx == 0)
        def _():
            for p in range(4):
                c[p, :, pl.ds(8, 40), :] = zc

        @pl.when(gx == nx - 1)
        def _():
            for p in range(36, 40):
                c[p, :, pl.ds(8, 40), :] = zc

    first40 = l40 == 0
    last40 = l40 == 127

    def coarse_sweep(c, v, lo, hi):
        def body(p, _):
            own = [c[p, h, pl.ds(8, 40), :] for h in range(2)]
            right = [pltpu.roll(own[h], 1, 1) for h in range(2)]
            left = [pltpu.roll(own[h], 127, 1) for h in range(2)]
            for h in range(2):
                total = c[p - 1, h, pl.ds(8, 40), :] + c[p + 1, h, pl.ds(8, 40), :]
                total = total + (c[p, h, pl.ds(7, 40), :] + c[p, h, pl.ds(9, 40), :])
                total = total + (own[h] + g2[p, h])
                total = total + jnp.where(first40, right[1 - h], right[h])
                total = total + jnp.where(last40, left[1 - h], left[h])
                v[p, h, pl.ds(8, 40), :] = total * kc[h]
            return 0

        lax.fori_loop(lo, hi, body, 0, unroll=2)
        clip(v)

    clip(ca)
    coarse_sweep(ca, cb, 1, 39)
    coarse_sweep(cb, ca, 2, 38)
    coarse_sweep(ca, cb, 3, 37)

    def prolong_z(n, _):
        i = 11 * n
        block = [cb[pl.ds(3 + i, 11), h, pl.ds(8, 40), :].reshape(440, 128) for h in range(2)]
        got = dot3(jnp.concatenate(block, axis=1), wp[...])
        for h in range(2):
            fz[pl.ds(i, 11), h] = got[:, 128 * h : 128 * h + 128].reshape(11, 40, 128)
        return 0

    lax.fori_loop(0, 3, prolong_z, 0)

    def prolong_y(j, slot):
        for h in range(2):
            here = fz[j, h, pl.ds(4, 32), :]
            wt[slot, h, pl.ds(0, 32, stride=2), :] = 0.5 * (fz[j, h, pl.ds(3, 32), :] + here)
            wt[slot, h, pl.ds(1, 32, stride=2), :] = here

    prolong_y(0, 0)

    def outgoing(x, n, h):
        return pltpu.make_async_copy(
            u2.at[pl.ds(3 + x, n), h, pl.ds(8, 64), :], out.at[pl.ds(x, n), :, pl.ds(128 * h, 128)], out_sem.at[h])

    def finish(i, _):
        slot = lax.rem(i + 1, 2)
        prolong_y(i + 1, slot)
        for h in range(2):
            here = wt[slot, h]
            mean = 0.5 * (wt[1 - slot, h] + here)
            u2[2 * i + 3, h, pl.ds(8, 64), :] = u2[2 * i + 3, h, pl.ds(8, 64), :] + mean
            u2[2 * i + 4, h, pl.ds(8, 64), :] = u2[2 * i + 4, h, pl.ds(8, 64), :] + here
        for h in range(2):
            outgoing(2 * i, 2, h).start()
        return 0

    lax.fori_loop(0, 32, finish, 0)
    for h in range(2):
        outgoing(0, 64, h).wait()
    sent(round0)
    sent(round1)
    for dx, dy, dz, copy in messages:
        pl.when(has_all(dx, dy, dz))(copy.wait_send)


def on_device(start_field, right_side):
    v = pltpu.VMEM
    scratch = [
        v((66, 2, 80, 128), F32), v((66, 2, 80, 128), F32), v((71, 2, 80, 128), F32),
        v((69, 2, 64, 128), F32), v((2, 64, 128), F32), v((2, 2, 64, 128), F32),
        v((2, 4, 96, 128), F32), v((34, 40, 512), F32), v((512, 256), BF16), v((256, 256), BF16),
        v((40, 40, 128), F32), v((40, 40, 128), F32), v((2, 3, 40, 128), F32), v((2, 3, 40, 128), F32),
        v((3, 40, 128), F32), v((40, 2, 40, 128), F32), v((40, 2, 56, 128), F32), v((40, 2, 56, 128), F32),
        v((33, 2, 40, 128), F32), v((2, 2, 64, 128), F32),
    ]
    scratch += [v((SEND[dx][1], SEND[dy][1], 128), F32) for dx, dy in XY8]
    scratch += [v((2, TSEND[dx][1], SEND[dy][1], 128), F32) for dx, dy in XY8]
    scratch += [v((2, TSEND[dx][1], SEND[dy][1], 128), F32) for dx, dy in XY]
    dma = pltpu.SemaphoreType.DMA
    scratch += [dma((4,)), dma((2,)), dma((2, 6)), dma((2, 6)), dma((8,)), dma((8,)), dma((8,)), dma((8,)),
                dma((9, 2)), dma((9, 2))]
    anywhere = pl.BlockSpec(memory_space=pl.ANY)
    return pl.pallas_call(
        kernel,
        out_shape=jax.ShapeDtypeStruct(start_field.shape, F32),
        in_specs=[anywhere, anywhere],
        out_specs=anywhere,
        scratch_shapes=scratch,
        compiler_params=pltpu.CompilerParams(
            collective_id=0, has_side_effects=True, vmem_limit_bytes=60 * 1024 * 1024),
    )(start_field, right_side)


def solution(mesh):
    placed = P("gx", "gy", "gz")
    return jax.shard_map(on_device, mesh=mesh, in_specs=(placed, placed), out_specs=placed, check_vma=False)
```

profile of v0, /device:TPU:10, one launch (start us, length us, event | category | flops | bytes accessed | tf_op | source)
XLA Modules:
  0.0 56.7 jit_solution(1626850410493593981)
XLA Ops:
  0.0 52.0 %shard_map.28 = f32[64,64,256]{2,1,0:T(8,128)} custom-call(f32[64,64,256]{2,1,0:T(8,128)} %s_in.1, f32[64,64,256]{2,1,0:T(8,128)} %b_in.1), custom_call_target="tpu_custom_call" | custom-call | tf_op jit(solution)/shard_map/pallas_call | solution.py:479
  52.0 4.7 %copy.4 = f32[64,64,256]{2,1,0:T(8,128)} copy(f32[64,64,256]{2,1,0:T(8,128)} %shard_map.28) | data formatting | bytes 8388608
where the time goes:
time: 57.5 us; the launch traced here: 56.7 us
  Pallas kernels  52 us (90%)
  local copies, waits for them, and re-layouts  4.7 us (8%)
    pallas_call x1, Pallas kernels, on_device(): pl.pallas_call(kernel, out_shape=jax.ShapeDtypeStruct(start_field.shape,...  52 us
    unnamed x1, local copies, waits for them, and re-layouts  4.7 us

commit v1 on v0

--- a/solution.py
+++ b/solution.py
@@ -11,6 +11,8 @@
 F32 = jnp.float32
 BF16 = jnp.bfloat16
 SEVENTH = 1.0 / 7.0
+UP, US, UE, UA, UR, UF = 8, 8, 8, 8, 2, 2
+UC = (8, 6, 7)
 AXES = ("gx", "gy", "gz")
 SEND = {-1: (3, 4), 0: (3, 34), 1: (32, 5)}
 LAND = {-1: 35, 0: 3, 1: 0}
@@ -33,12 +35,12 @@
     return (parts[2] + parts[1]) + parts[0]
 
 
-def kernel(s_in, b_in, out, *scratch):
-    (u0, u1, u2, bv, ez, zr, at, qb, wr, wp, gm, gs, lh, ls, kc, g2, ca, cb, fz, wt) = scratch[:20]
-    rm = scratch[20:28]
-    rl = scratch[28:36]
-    rz = scratch[36:45]
-    load_sem, out_sem, f_send, f_recv, m_send, m_recv, l_send, l_recv, z_send, z_recv = scratch[45:]
+def kernel(s_in, b_in, u2, fz, *scratch):
+    (u0, u1, bv, ez, zr, at, qb, wr, wp, gm, gs, lh, ls, kc, g2, ca, cb) = scratch[:17]
+    rm = scratch[17:25]
+    rl = scratch[25:33]
+    rz = scratch[33:42]
+    load_sem, f_send, f_recv, m_send, m_recv, l_send, l_recv, z_send, z_recv = scratch[42:]
 
     gx, gy, gz = (lax.axis_index(a) for a in AXES)
     nx, ny, nz = (lax.axis_size(a) for a in AXES)
@@ -211,7 +213,7 @@
     def pack(x, packed):
         return pack_face(u0[x + 1, 0, pl.ds(8, 64), :], u0[x + 1, 1, pl.ds(8, 64), :], x, packed)
 
-    ez[0] = lax.fori_loop(0, 64, pack, jnp.zeros((64, 128), F32), unroll=4)
+    ez[0] = lax.fori_loop(0, 64, pack, jnp.zeros((64, 128), F32), unroll=UP)
     start(round0[4:])
 
     def sweep(r, u, off, v, voff):
@@ -239,7 +241,7 @@
             return packed
 
         init = jnp.zeros((64, 128), F32) if r == 0 else jnp.int32(0)
-        return lax.fori_loop(0, 64, body, init, unroll=2)
+        return lax.fori_loop(0, 64, body, init, unroll=US)
 
     loads[2].wait()
     loads[3].wait()
@@ -271,9 +273,11 @@
             qb[i, :, pl.ds(256 + 128 * h, 128)] = 0.25 * beside + 0.5 * a1[2]
         return 0
 
-    lax.fori_loop(0, 34, restrict, 0, unroll=2)
+    lax.fori_loop(0, 34, restrict, 0, unroll=UR)
 
     gm[...] = jnp.zeros(gm.shape, F32)
+    for p in (0, 1, 2, 37, 38, 39):
+        g2[p, 1] = zero40
     gs[...] = jnp.zeros(gs.shape, F32)
 
     def restrict_z(n, _):
@@ -289,7 +293,7 @@
 
     edge40 = l40 >= 124
     oct40 = l40 // 8
-    for t, (lo, hi) in enumerate(((3, 16), (16, 32), (32, 37))):
+    for t, (lo, hi) in enumerate(((0, 16), (16, 32), (32, 40))):
 
         def pack_ends(p, ends):
             main, halo = gm[p], g2[p, 1]
@@ -301,7 +305,7 @@
                 jnp.where(here, pltpu.roll(jnp.where(edge40, main, halo), shift, 1), ends[1]),
             )
 
-        ends = lax.fori_loop(lo, hi, pack_ends, (zero40, zero40))
+        ends = lax.fori_loop(lo, hi, pack_ends, (zero40, zero40), unroll=UE)
         for k in range(2):
             lh[k, t] = ends[k]
             ls[k, t] = ends[k]
@@ -357,7 +361,7 @@
                     ls[k, tl + t, rows, :] = ls[k, tl + t, rows, :] + src[k, t]
 
     begin40 = l40 < 4
-    zpad = jnp.zeros((40, 2, 8, 128), F32)
+    zpad = jnp.zeros((42, 2, 8, 128), F32)
     for c in (ca, cb):
         c[:, :, pl.ds(0, 8), :] = zpad
         c[:, :, pl.ds(48, 8), :] = zpad
@@ -376,7 +380,7 @@
         ca[p, 1, pl.ds(8, 40), :] = halo * kc[1]
         return 0
 
-    lax.fori_loop(0, 40, assemble, 0, unroll=2)
+    lax.fori_loop(0, 40, assemble, 0, unroll=UA)
 
     zc = jnp.zeros((2, 40, 128), F32)
 
@@ -394,7 +398,7 @@
     first40 = l40 == 0
     last40 = l40 == 127
 
-    def coarse_sweep(c, v, lo, hi):
+    def coarse_sweep(c, v, lo, hi, unroll):
         def body(p, _):
             own = [c[p, h, pl.ds(8, 40), :] for h in range(2)]
             right = [pltpu.roll(own[h], 1, 1) for h in range(2)]
@@ -408,13 +412,13 @@
                 v[p, h, pl.ds(8, 40), :] = total * kc[h]
             return 0
 
-        lax.fori_loop(lo, hi, body, 0, unroll=2)
+        lax.fori_loop(lo, hi, body, 0, unroll=unroll)
         clip(v)
 
     clip(ca)
-    coarse_sweep(ca, cb, 1, 39)
-    coarse_sweep(cb, ca, 2, 38)
-    coarse_sweep(ca, cb, 3, 37)
+    coarse_sweep(ca, cb, 1, 41, UC[0])
+    coarse_sweep(cb, ca, 2, 38, UC[1])
+    coarse_sweep(ca, cb, 3, 38, UC[2])
 
     def prolong_z(n, _):
         i = 11 * n
@@ -426,6 +430,13 @@
 
     lax.fori_loop(0, 3, prolong_z, 0)
 
+    sent(round0)
+    sent(round1)
+    for dx, dy, dz, copy in messages:
+        pl.when(has_all(dx, dy, dz))(copy.wait_send)
+
+
+def finish_kernel(u2, fz, out, ot, wt, out_sem):
     def prolong_y(j, slot):
         for h in range(2):
             here = fz[j, h, pl.ds(4, 32), :]
@@ -436,7 +447,7 @@
 
     def outgoing(x, n, h):
         return pltpu.make_async_copy(
-            u2.at[pl.ds(3 + x, n), h, pl.ds(8, 64), :], out.at[pl.ds(x, n), :, pl.ds(128 * h, 128)], out_sem.at[h])
+            ot.at[pl.ds(x, n), h], out.at[pl.ds(x, n), :, pl.ds(128 * h, 128)], out_sem.at[h])
 
     def finish(i, _):
         slot = lax.rem(i + 1, 2)
@@ -444,47 +455,51 @@
         for h in range(2):
             here = wt[slot, h]
             mean = 0.5 * (wt[1 - slot, h] + here)
-            u2[2 * i + 3, h, pl.ds(8, 64), :] = u2[2 * i + 3, h, pl.ds(8, 64), :] + mean
-            u2[2 * i + 4, h, pl.ds(8, 64), :] = u2[2 * i + 4, h, pl.ds(8, 64), :] + here
+            ot[2 * i, h] = u2[2 * i + 3, h, pl.ds(8, 64), :] + mean
+            ot[2 * i + 1, h] = u2[2 * i + 4, h, pl.ds(8, 64), :] + here
         for h in range(2):
             outgoing(2 * i, 2, h).start()
         return 0
 
-    lax.fori_loop(0, 32, finish, 0)
+    lax.fori_loop(0, 32, finish, 0, unroll=UF)
     for h in range(2):
         outgoing(0, 64, h).wait()
-    sent(round0)
-    sent(round1)
-    for dx, dy, dz, copy in messages:
-        pl.when(has_all(dx, dy, dz))(copy.wait_send)
 
 
 def on_device(start_field, right_side):
     v = pltpu.VMEM
     scratch = [
-        v((66, 2, 80, 128), F32), v((66, 2, 80, 128), F32), v((71, 2, 80, 128), F32),
+        v((66, 2, 80, 128), F32), v((66, 2, 80, 128), F32),
         v((69, 2, 64, 128), F32), v((2, 64, 128), F32), v((2, 2, 64, 128), F32),
         v((2, 4, 96, 128), F32), v((34, 40, 512), F32), v((512, 256), BF16), v((256, 256), BF16),
         v((40, 40, 128), F32), v((40, 40, 128), F32), v((2, 3, 40, 128), F32), v((2, 3, 40, 128), F32),
-        v((3, 40, 128), F32), v((40, 2, 40, 128), F32), v((40, 2, 56, 128), F32), v((40, 2, 56, 128), F32),
-        v((33, 2, 40, 128), F32), v((2, 2, 64, 128), F32),
+        v((3, 40, 128), F32), v((42, 2, 40, 128), F32), v((42, 2, 56, 128), F32), v((42, 2, 56, 128), F32),
     ]
     scratch += [v((SEND[dx][1], SEND[dy][1], 128), F32) for dx, dy in XY8]
     scratch += [v((2, TSEND[dx][1], SEND[dy][1], 128), F32) for dx, dy in XY8]
     scratch += [v((2, TSEND[dx][1], SEND[dy][1], 128), F32) for dx, dy in XY]
     dma = pltpu.SemaphoreType.DMA
-    scratch += [dma((4,)), dma((2,)), dma((2, 6)), dma((2, 6)), dma((8,)), dma((8,)), dma((8,)), dma((8,)),
+    scratch += [dma((4,)), dma((2, 6)), dma((2, 6)), dma((8,)), dma((8,)), dma((8,)), dma((8,)),
                 dma((9, 2)), dma((9, 2))]
-    anywhere = pl.BlockSpec(memory_space=pl.ANY)
-    return pl.pallas_call(
+    anywhere = pl.BlockSpec(memory_space=pltpu.HBM)
+    vmem = pl.BlockSpec(memory_space=pltpu.VMEM)
+    smoothed, correction = pl.pallas_call(
         kernel,
-        out_shape=jax.ShapeDtypeStruct(start_field.shape, F32),
+        out_shape=(v((71, 2, 80, 128), F32), v((33, 2, 40, 128), F32)),
         in_specs=[anywhere, anywhere],
-        out_specs=anywhere,
+        out_specs=(vmem, vmem),
         scratch_shapes=scratch,
         compiler_params=pltpu.CompilerParams(
-            collective_id=0, has_side_effects=True, vmem_limit_bytes=60 * 1024 * 1024),
+            collective_id=0, has_side_effects=True, vmem_limit_bytes=54 * 1024 * 1024),
     )(start_field, right_side)
+    return pl.pallas_call(
+        finish_kernel,
+        out_shape=jax.ShapeDtypeStruct(start_field.shape, F32),
+        in_specs=[vmem, vmem],
+        out_specs=anywhere,
+        scratch_shapes=[v((64, 2, 64, 128), F32), v((2, 2, 64, 128), F32), dma((2,))],
+        compiler_params=pltpu.CompilerParams(vmem_limit_bytes=12 * 1024 * 1024),
+    )(smoothed, correction)
 
 
 def solution(mesh):

time: 57.5 us -> 45.6 us (0.79)
  the two profiles are of different devices: /device:TPU:10 before, /device:TPU:29 now
where the time goes in v1:
time: 45.6 us; the launch traced here: 45.5 us
  Pallas kernels  45.5 us (100%)
    pallas_call x1, Pallas kernels, on_device(): pl.pallas_call(kernel, out_shape=(v((71, 2, 80, 128), F32), v((33, 2, 40,...  43.5 us
    pallas_call x1, Pallas kernels, on_device(): pl.pallas_call(finish_kernel, out_shape=jax.ShapeDtypeStruct(start_field....  2.01 us

profile of v1, /device:TPU:29, one launch (start us, length us, event | category | flops | bytes accessed | tf_op | source)
XLA Modules:
  0.0 45.5 jit_solution(16625197054131999086)
XLA Ops:
  0.0 43.5 %shard_map.28 = (f32[71,2,80,128]{3,2,1,0:T(8,128)S(1)}, f32[33,2,40,128]{3,2,1,0:T(8,128)S(1)}) custom-call(f32[64,64,256]{2,1,0:T(8,128)} %s_in.1, f32[64,64,256]{2,1,0:T(8,128)} %b_in.1), custom_call_target="tpu_custom_call" | custom-call | tf_op jit(solution)/shard_map/pallas_call | solution.py:486
  43.5 2.0 %shard_map.29 = f32[64,64,256]{2,1,0:T(8,128)} custom-call(f32[71,2,80,128]{3,2,1,0:T(8,128)S(1)} %get-tuple-element.7.u2, f32[33,2,40,128]{3,2,1,0:T(8,128)S(1)} %get-tuple-element.8.fz), custom_call_target="tpu_custom_call" | custom-call | tf_op jit(solution)/shard_map/pallas_call | solution.py:495

commit v2 on v1

--- a/solution.py
+++ b/solution.py
@@ -11,7 +11,8 @@
 F32 = jnp.float32
 BF16 = jnp.bfloat16
 SEVENTH = 1.0 / 7.0
-UP, US, UE, UA, UR, UF = 8, 8, 8, 8, 2, 2
+UE, UA, UF = 8, 8, 2
+NI, GI, GO = 6, 4, 8
 UC = (8, 6, 7)
 AXES = ("gx", "gy", "gz")
 SEND = {-1: (3, 4), 0: (3, 34), 1: (32, 5)}
@@ -36,11 +37,11 @@
 
 
 def kernel(s_in, b_in, u2, fz, *scratch):
-    (u0, u1, bv, ez, zr, at, qb, wr, wp, gm, gs, lh, ls, kc, g2, ca, cb) = scratch[:17]
-    rm = scratch[17:25]
-    rl = scratch[25:33]
-    rz = scratch[33:42]
-    load_sem, f_send, f_recv, m_send, m_recv, l_send, l_recv, z_send, z_recv = scratch[42:]
+    (u0, u1, bv, ez, zr, at, qb, wr, wp, gm, gs, lh, ls, kc, g2, ca, cb, zs) = scratch[:18]
+    rm = scratch[18:26]
+    rl = scratch[26:34]
+    rz = scratch[34:43]
+    load_sem, f_send, f_recv, m_send, m_recv, l_send, l_recv, z_send, z_recv, h_send, h_recv = scratch[43:]
 
     gx, gy, gz = (lax.axis_index(a) for a in AXES)
     nx, ny, nz = (lax.axis_size(a) for a in AXES)
@@ -70,8 +71,8 @@
     for h in range(2):
         lanes = pl.ds(128 * h, 128)
         loads.append(pltpu.make_async_copy(b_in.at[:, :, lanes], bv.at[pl.ds(2, 64), h], load_sem.at[2 + h]))
-    for c in loads:
-        c.start()
+    loads[0].start()
+    loads[1].start()
 
     barrier = pltpu.get_barrier_semaphore()
     count = jnp.int32(0)
@@ -162,9 +163,18 @@
     high_z = jnp.where(gz < nz - 1, 4, 0)
     rows_in = jnp.where((r40 >= low_y) & (r40 < high_y), SEVENTH, zero40)
     kc[0] = rows_in
+    for p in (0, 1, 2, 37, 38, 39):
+        gm[p] = zero40
+        gs[p] = zero40
+        g2[p, 1] = zero40
     kc[1] = jnp.where((l40 >= low_z) | (l40 < high_z), rows_in, zero40)
     topy = (gy == ny - 1).astype(F32)
     kc[2] = 0.5 - jnp.where(r40 == 35, 0.25 * topy, zero40)
+
+    zpad = jnp.zeros((42, 2, 8, 128), F32)
+    for c in (ca, cb):
+        c[:, :, pl.ds(0, 8), :] = zpad
+        c[:, :, pl.ds(48, 8), :] = zpad
 
     def faces(r, u):
         x_in = (slice(None), pl.ds(8, 64), slice(None))
@@ -203,53 +213,98 @@
 
     loads[0].wait()
     loads[1].wait()
+    loads[2].start()
+    loads[3].start()
     pl.semaphore_wait(barrier, count)
     start(round0[:4])
 
-    def pack_face(low, high, x, packed):
-        both = jnp.where(first, low, high)
-        return jnp.where(group == x, pltpu.roll(both, 2 * x, 1), packed)
-
-    def pack(x, packed):
-        return pack_face(u0[x + 1, 0, pl.ds(8, 64), :], u0[x + 1, 1, pl.ds(8, 64), :], x, packed)
-
-    ez[0] = lax.fori_loop(0, 64, pack, jnp.zeros((64, 128), F32), unroll=UP)
+    group8 = group[:8]
+    first8, last8 = first[:8], last[:8]
+
+    def pack(n, packed):
+        for j in range(8):
+            x = 8 * n + j
+            both = jnp.where(first, u0[x + 1, 0, pl.ds(8, 64), :], u0[x + 1, 1, pl.ds(8, 64), :])
+            packed = jnp.where(group == x, pltpu.roll(both, 2 * x, 1), packed)
+        return packed
+
+    ez[0] = lax.fori_loop(0, 8, pack, jnp.zeros((64, 128), F32))
+    ez[1] = jnp.zeros((64, 128), F32)
     start(round0[4:])
 
-    def sweep(r, u, off, v, voff):
+    def beside_z(r, u, starts, x0, group_size):
+        halo = [zr[r, 0, pl.ds(y, 8), :] for y in starts]
+        for j in range(group_size):
+            x = x0 + j
+            shift = lax.rem(128 - 2 * x, 128)
+            for k, y in enumerate(starts):
+                side = pltpu.roll(halo[k], shift, 1)
+                c = [u[x + 1, h, pl.ds(8 + y, 8), :] for h in range(2)]
+                right = [pltpu.roll(c[h], 1, 1) for h in range(2)]
+                left = [pltpu.roll(c[h], 127, 1) for h in range(2)]
+                zs[j, k, 0] = jnp.where(first8, side, right[0]) + jnp.where(last8, left[1], left[0])
+                zs[j, k, 1] = jnp.where(first8, right[0], right[1]) + jnp.where(last8, side, left[1])
+
+    def pack_ends_of(v, starts, x0, group_size):
+        packed = [ez[1, pl.ds(y, 8), :] for y in starts]
+        for j in range(group_size):
+            x = x0 + j
+            here = group8 == x
+            for k, y in enumerate(starts):
+                both = jnp.where(first8, v[x + 1, 0, pl.ds(8 + y, 8), :], v[x + 1, 1, pl.ds(8 + y, 8), :])
+                packed[k] = jnp.where(here, pltpu.roll(both, 2 * x, 1), packed[k])
+        for k, y in enumerate(starts):
+            ez[1, pl.ds(y, 8), :] = packed[k]
+
+    def relax(u, v, off, starts, x0, group_size):
+        def planes(p):
+            return [[u[p, h, pl.ds(8 + y, 8), :] for h in range(2)] for y in starts]
+
+        before, here = planes(x0), planes(x0 + 1)
+        for j in range(group_size):
+            x = x0 + j
+            after = planes(x + 2)
+            for k, y in enumerate(starts):
+                for h in range(2):
+                    total = (before[k][h] + after[k][h]) + (here[k][h] + bv[x + 2, h, pl.ds(y, 8), :])
+                    total = total + (u[x + 1, h, pl.ds(7 + y, 8), :] + u[x + 1, h, pl.ds(9 + y, 8), :])
+                    v[x + off, h, pl.ds(8 + y, 8), :] = (total + zs[j, k, h]) * SEVENTH
+            before, here = here, after
+
+    def pipelined(r, u, v, off, count, place, group_size):
+        beside_z(r, u, *place(0), group_size)
+
+        def body(n, _):
+            if r == 0:
+                pack_ends_of(v, *place(jnp.maximum(n - 1, 0)), group_size)
+            relax(u, v, off, *place(n), group_size)
+            beside_z(r, u, *place(jnp.minimum(n + 1, count - 1)), group_size)
+            return 0
+
+        lax.fori_loop(0, count, body, 0)
+        if r == 0:
+            pack_ends_of(v, *place(count - 1), group_size)
+
+    def sweep(r, copies, u, v, off):
+        arrive(copies[4:])
         even = lax.rem(lane, 2) == 0
-        halo = jnp.where(even, pltpu.roll(zr[r, 0], 1, 1), pltpu.roll(zr[r, 1], 127, 1))
-        zr[r, 0] = halo
-
-        def body(x, packed):
-            side = pltpu.roll(zr[r, 0], lax.rem(128 - 2 * x, 128), 1)
-            c = [u[x + off, h, pl.ds(8, 64), :] for h in range(2)]
-            right = [pltpu.roll(c[h], 1, 1) for h in range(2)]
-            left = [pltpu.roll(c[h], 127, 1) for h in range(2)]
-            below = [jnp.where(first, side, right[0]), jnp.where(first, right[0], right[1])]
-            above = [jnp.where(last, left[1], left[0]), jnp.where(last, side, left[1])]
-            new = []
-            for h in range(2):
-                total = u[x + off - 1, h, pl.ds(8, 64), :] + u[x + off + 1, h, pl.ds(8, 64), :]
-                total = total + (u[x + off, h, pl.ds(7, 64), :] + u[x + off, h, pl.ds(9, 64), :])
-                total = total + (c[h] + bv[x + 2, h])
-                total = (total + (below[h] + above[h])) * SEVENTH
-                v[x + voff, h, pl.ds(8, 64), :] = total
-                new.append(total)
-            if r == 0:
-                packed = pack_face(new[0], new[1], x, packed)
-            return packed
-
-        init = jnp.zeros((64, 128), F32) if r == 0 else jnp.int32(0)
-        return lax.fori_loop(0, 64, body, init, unroll=US)
+        zr[r, 0] = jnp.where(even, pltpu.roll(zr[r, 0], 1, 1), pltpu.roll(zr[r, 1], 127, 1))
+        arrive(copies[:2])
+        every = 64 // GI
+
+        def inner(n):
+            y = 8 + 8 * NI * (n // every)
+            return [pl.multiple_of(y + 8 * k, 8) for k in range(NI)], GI * lax.rem(n, every)
+
+        pipelined(r, u, v, off, (6 // NI) * every, inner, GI)
+        arrive(copies[2:4])
+        pipelined(r, u, v, off, 64 // GO, lambda n: ([0, 56], GO * n), GO)
 
     loads[2].wait()
     loads[3].wait()
-    arrive(round0)
-    ez[1] = sweep(0, u0, 1, u1, 1)
+    sweep(0, round0, u0, u1, 1)
     start(round1)
-    arrive(round1)
-    sweep(1, u1, 1, u2, 3)
+    sweep(1, round1, u1, u2, 3)
 
     topx = gx == nx - 1
 
@@ -273,15 +328,10 @@
             qb[i, :, pl.ds(256 + 128 * h, 128)] = 0.25 * beside + 0.5 * a1[2]
         return 0
 
-    lax.fori_loop(0, 34, restrict, 0, unroll=UR)
-
-    gm[...] = jnp.zeros(gm.shape, F32)
-    for p in (0, 1, 2, 37, 38, 39):
-        g2[p, 1] = zero40
-    gs[...] = jnp.zeros(gs.shape, F32)
-
-    def restrict_z(n, _):
+
+    def restrict_half(n, _):
         i = 17 * n
+        lax.fori_loop(i, i + 17, restrict, 0)
         got = dot3(qb[pl.ds(i, 17)].reshape(680, 512), wr[...])
         main = got[:, :128].reshape(17, 40, 128)
         gm[pl.ds(i + 3, 17)] = main
@@ -289,7 +339,34 @@
         g2[pl.ds(i + 3, 17), 1] = got[:, 128:].reshape(17, 40, 128)
         return 0
 
-    lax.fori_loop(0, 2, restrict_z, 0)
+    def half_message(n, dy):
+        ya, yn = SEND[dy]
+        e = 0 if dy < 0 else 1
+        return pltpu.make_async_remote_copy(
+            src_ref=gm.at[pl.ds(3 + 17 * n, 17), pl.ds(ya, yn), :],
+            dst_ref=rm[XY8.index((0, dy))].at[pl.ds(17 * n, 17)],
+            send_sem=h_send.at[n, e], recv_sem=h_recv.at[n, e],
+            device_id=target(0, dy, 0), device_id_type=MESH)
+
+    mains = []
+    for n, (dx, dy) in enumerate(XY8):
+        if dx:
+            (xa, xn), (ya, yn) = SEND[dx], SEND[dy]
+            mains.append((dx, dy, n, pltpu.make_async_remote_copy(
+                src_ref=gm.at[pl.ds(xa, xn), pl.ds(ya, yn), :], dst_ref=rm[n],
+                send_sem=m_send.at[n], recv_sem=m_recv.at[n], device_id=target(dx, dy, 0), device_id_type=MESH)))
+    mains.sort(key=lambda m: abs(m[1]))
+
+    def half(n, _):
+        restrict_half(n, 0)
+        for dy in (-1, 1):
+            pl.when(has("gy", dy))(lambda: half_message(n, dy).start())
+        for dx, dy, _, copy in mains:
+            ready = n == (0 if dx < 0 else 1)
+            pl.when(jnp.logical_and(ready, has_all(dx, dy, 0)))(copy.start)
+        return 0
+
+    lax.fori_loop(0, 2, half, 0)
 
     edge40 = l40 >= 124
     oct40 = l40 // 8
@@ -312,60 +389,59 @@
 
     messages = []
     for n, (dx, dy) in enumerate(XY8):
-        (xa, xn), (ya, yn) = SEND[dx], SEND[dy]
-        (ta, tn) = TSEND[dx]
-        to = target(dx, dy, 0)
-        messages.append((dx, dy, 0, pltpu.make_async_remote_copy(
-            src_ref=gm.at[pl.ds(xa, xn), pl.ds(ya, yn), :], dst_ref=rm[n],
-            send_sem=m_send.at[n], recv_sem=m_recv.at[n], device_id=to, device_id_type=MESH)))
-        messages.append((dx, dy, 0, pltpu.make_async_remote_copy(
+        ya, yn = SEND[dy]
+        ta, tn = TSEND[dx]
+        messages.append((dx, dy, 0, n, pltpu.make_async_remote_copy(
             src_ref=lh.at[:, pl.ds(ta, tn), pl.ds(ya, yn), :], dst_ref=rl[n],
-            send_sem=l_send.at[n], recv_sem=l_recv.at[n], device_id=to, device_id_type=MESH)))
+            send_sem=l_send.at[n], recv_sem=l_recv.at[n], device_id=target(dx, dy, 0), device_id_type=MESH)))
     for n, (dx, dy) in enumerate(XY):
         ya, yn = SEND[dy]
         ta, tn = TSEND[dx]
         for dz in (-1, 1):
             end = 1 if dz > 0 else 0
-            messages.append((dx, dy, dz, pltpu.make_async_remote_copy(
+            messages.append((dx, dy, dz, n, pltpu.make_async_remote_copy(
                 src_ref=lh.at[end, pl.ds(ta, tn), pl.ds(ya, yn), :], dst_ref=rz[n].at[1 - end],
                 send_sem=z_send.at[n, end], recv_sem=z_recv.at[n, end],
                 device_id=target(dx, dy, dz), device_id_type=MESH)))
-    for dx, dy, dz, copy in messages:
+    messages.sort(key=lambda m: (abs(m[0]) + abs(m[1]) + abs(m[2])))
+    for dx, dy, dz, _, copy in messages:
         pl.when(has_all(dx, dy, dz))(copy.start)
 
-    for n, (dx, dy, dz, copy) in enumerate(messages):
-        xn, yn, tn = SEND[dx][1], SEND[dy][1], TSEND[dx][1]
-        xl, yl, tl = LAND[dx], LAND[dy], TLAND[dx]
-
-        @pl.when(has_all(-dx, -dy, -dz))
-        def _():
-            copy.wait_recv()
-            rows = pl.ds(yl, yn)
-            if dz == 0 and n % 2 == 0:
-                src = rm[n // 2]
-
-                def add(p, _):
-                    gs[xl + p, rows, :] = gs[xl + p, rows, :] + src[p]
-                    return 0
-
-                lax.fori_loop(0, xn, add, 0)
-            elif dz == 0:
-                src = rl[n // 2]
-                for k in range(2):
-                    for t in range(tn):
-                        ls[k, tl + t, rows, :] = ls[k, tl + t, rows, :] + src[k, t]
-            else:
-                k = 0 if dz > 0 else 1
-                src = rz[(n - 16) // 2]
-                for t in range(tn):
-                    ls[k, tl + t, rows, :] = ls[k, tl + t, rows, :] + src[k, t]
+    def add_main(dx, dy, n):
+        xn, xl = SEND[dx][1], LAND[dx]
+        rows = pl.ds(LAND[dy], SEND[dy][1])
+
+        def add(p, _):
+            gs[xl + p, rows, :] = gs[xl + p, rows, :] + rm[n][p]
+            return 0
+
+        lax.fori_loop(0, xn, add, 0, unroll=min(xn, 17))
+
+    def take_half(dy):
+        half_message(0, dy).wait_recv()
+        half_message(1, dy).wait_recv()
+        add_main(0, dy, XY8.index((0, dy)))
+
+    def take_main(dx, dy, n, copy):
+        copy.wait_recv()
+        add_main(dx, dy, n)
+
+    def take_ends(dx, dy, dz, n, copy):
+        copy.wait_recv()
+        rows, tl = pl.ds(LAND[dy], SEND[dy][1]), TLAND[dx]
+        for k in (0, 1) if dz == 0 else (0,) if dz > 0 else (1,):
+            src = rl[n] if dz == 0 else rz[n]
+            for t in range(TSEND[dx][1]):
+                ls[k, tl + t, rows, :] = ls[k, tl + t, rows, :] + src[k, t]
+
+    for dy in (-1, 1):
+        pl.when(has("gy", -dy))(functools.partial(take_half, dy))
+    for dx, dy, n, copy in mains:
+        pl.when(has_all(-dx, -dy, 0))(functools.partial(take_main, dx, dy, n, copy))
+    for dx, dy, dz, n, copy in messages:
+        pl.when(has_all(-dx, -dy, -dz))(functools.partial(take_ends, dx, dy, dz, n, copy))
 
     begin40 = l40 < 4
-    zpad = jnp.zeros((42, 2, 8, 128), F32)
-    for c in (ca, cb):
-        c[:, :, pl.ds(0, 8), :] = zpad
-        c[:, :, pl.ds(48, 8), :] = zpad
-
     def assemble(p, _):
         t = p // 16
         q = p - 16 * t
@@ -398,21 +474,28 @@
     first40 = l40 == 0
     last40 = l40 == 127
 
-    def coarse_sweep(c, v, lo, hi, unroll):
-        def body(p, _):
-            own = [c[p, h, pl.ds(8, 40), :] for h in range(2)]
-            right = [pltpu.roll(own[h], 1, 1) for h in range(2)]
-            left = [pltpu.roll(own[h], 127, 1) for h in range(2)]
-            for h in range(2):
-                total = c[p - 1, h, pl.ds(8, 40), :] + c[p + 1, h, pl.ds(8, 40), :]
-                total = total + (c[p, h, pl.ds(7, 40), :] + c[p, h, pl.ds(9, 40), :])
-                total = total + (own[h] + g2[p, h])
-                total = total + jnp.where(first40, right[1 - h], right[h])
-                total = total + jnp.where(last40, left[1 - h], left[h])
-                v[p, h, pl.ds(8, 40), :] = total * kc[h]
+    def coarse_sweep(c, v, lo, hi, many):
+        def planes(p):
+            return [c[p, h, pl.ds(8, 40), :] for h in range(2)]
+
+        def body(n, _):
+            p0 = lo + many * n
+            before, own = planes(p0 - 1), planes(p0)
+            for j in range(many):
+                p = p0 + j
+                after = planes(p + 1)
+                right = [pltpu.roll(own[h], 1, 1) for h in range(2)]
+                left = [pltpu.roll(own[h], 127, 1) for h in range(2)]
+                for h in range(2):
+                    total = (before[h] + after[h]) + (own[h] + g2[p, h])
+                    total = total + (c[p, h, pl.ds(7, 40), :] + c[p, h, pl.ds(9, 40), :])
+                    total = total + jnp.where(first40, right[1 - h], right[h])
+                    total = total + jnp.where(last40, left[1 - h], left[h])
+                    v[p, h, pl.ds(8, 40), :] = total * kc[h]
+                before, own = own, after
             return 0
 
-        lax.fori_loop(lo, hi, body, 0, unroll=unroll)
+        lax.fori_loop(0, (hi - lo) // many, body, 0)
         clip(v)
 
     clip(ca)
@@ -432,7 +515,12 @@
 
     sent(round0)
     sent(round1)
-    for dx, dy, dz, copy in messages:
+    for n in range(2):
+        for dy in (-1, 1):
+            pl.when(has("gy", dy))(half_message(n, dy).wait_send)
+    for dx, dy, n, copy in mains:
+        pl.when(has_all(dx, dy, 0))(copy.wait_send)
+    for dx, dy, dz, n, copy in messages:
         pl.when(has_all(dx, dy, dz))(copy.wait_send)
 
 
@@ -474,13 +562,14 @@
         v((2, 4, 96, 128), F32), v((34, 40, 512), F32), v((512, 256), BF16), v((256, 256), BF16),
         v((40, 40, 128), F32), v((40, 40, 128), F32), v((2, 3, 40, 128), F32), v((2, 3, 40, 128), F32),
         v((3, 40, 128), F32), v((42, 2, 40, 128), F32), v((42, 2, 56, 128), F32), v((42, 2, 56, 128), F32),
+        v((max(GI, GO), max(NI, 2), 2, 8, 128), F32),
     ]
     scratch += [v((SEND[dx][1], SEND[dy][1], 128), F32) for dx, dy in XY8]
     scratch += [v((2, TSEND[dx][1], SEND[dy][1], 128), F32) for dx, dy in XY8]
     scratch += [v((2, TSEND[dx][1], SEND[dy][1], 128), F32) for dx, dy in XY]
     dma = pltpu.SemaphoreType.DMA
     scratch += [dma((4,)), dma((2, 6)), dma((2, 6)), dma((8,)), dma((8,)), dma((8,)), dma((8,)),
-                dma((9, 2)), dma((9, 2))]
+                dma((9, 2)), dma((9, 2)), dma((2, 2)), dma((2, 2))]
     anywhere = pl.BlockSpec(memory_space=pltpu.HBM)
     vmem = pl.BlockSpec(memory_space=pltpu.VMEM)
     smoothed, correction = pl.pallas_call(

time: 45.6 us -> 42.9 us (0.941)
  the two profiles are of different devices: /device:TPU:29 before, /device:TPU:10 now
where the time goes in v2:
time: 42.9 us; the launch traced here: 42.7 us
  Pallas kernels  42.7 us (100%)
    pallas_call x1, Pallas kernels, on_device(): pl.pallas_call(kernel, out_shape=(v((71, 2, 80, 128), F32), v((33, 2, 40,...  40.7 us
    pallas_call x1, Pallas kernels, on_device(): pl.pallas_call(finish_kernel, out_shape=jax.ShapeDtypeStruct(start_field....  2.01 us

profile of v2, /device:TPU:10, one launch (start us, length us, event | category | flops | bytes accessed | tf_op | source)
XLA Modules:
  0.0 42.7 jit_solution(10018210845244671248)
XLA Ops:
  0.0 40.7 %shard_map.28 = (f32[71,2,80,128]{3,2,1,0:T(8,128)S(1)}, f32[33,2,40,128]{3,2,1,0:T(8,128)S(1)}) custom-call(f32[64,64,256]{2,1,0:T(8,128)} %s_in.1, f32[64,64,256]{2,1,0:T(8,128)} %b_in.1), custom_call_target="tpu_custom_call" | custom-call | tf_op jit(solution)/shard_map/pallas_call | solution.py:575
  40.7 2.0 %shard_map.29 = f32[64,64,256]{2,1,0:T(8,128)} custom-call(f32[71,2,80,128]{3,2,1,0:T(8,128)S(1)} %get-tuple-element.7.u2, f32[33,2,40,128]{3,2,1,0:T(8,128)S(1)} %get-tuple-element.8.fz), custom_call_target="tpu_custom_call" | custom-call | tf_op jit(solution)/shard_map/pallas_call | solution.py:584

commit v3 on v2

--- a/solution.py
+++ b/solution.py
@@ -12,7 +12,7 @@
 BF16 = jnp.bfloat16
 SEVENTH = 1.0 / 7.0
 UE, UA, UF = 8, 8, 2
-NI, GI, GO = 6, 4, 8
+NI, GI, GH = 4, 8, 8
 UC = (8, 6, 7)
 AXES = ("gx", "gy", "gz")
 SEND = {-1: (3, 4), 0: (3, 34), 1: (32, 5)}
@@ -37,11 +37,11 @@
 
 
 def kernel(s_in, b_in, u2, fz, *scratch):
-    (u0, u1, bv, ez, zr, at, qb, wr, wp, gm, gs, lh, ls, kc, g2, ca, cb, zs) = scratch[:18]
-    rm = scratch[18:26]
-    rl = scratch[26:34]
-    rz = scratch[34:43]
-    load_sem, f_send, f_recv, m_send, m_recv, l_send, l_recv, z_send, z_recv, h_send, h_recv = scratch[43:]
+    (u0, u1, bv, ez, zr, at, qb, wr, wp, gm, gs, lh, ls, kc, g2, ca, cb, zs, hx, hy) = scratch[:20]
+    rm = scratch[20:28]
+    rl = scratch[28:36]
+    rz = scratch[36:45]
+    load_sem, f_send, f_recv, m_send, m_recv, l_send, l_recv, z_send, z_recv, h_send, h_recv = scratch[45:]
 
     gx, gy, gz = (lax.axis_index(a) for a in AXES)
     nx, ny, nz = (lax.axis_size(a) for a in AXES)
@@ -92,43 +92,42 @@
 
     zplane = jnp.zeros((2, 80, 128), F32)
     zrow = jnp.zeros((1, 128), F32)
-
-    @pl.when(gx == 0)
-    def _():
-        u0[0] = zplane
-        u1[0] = zplane
-
-    @pl.when(gx == nx - 1)
-    def _():
-        u0[65] = zplane
-        u1[65] = zplane
-
-    def zero_rows(row):
+    for u in (u0, u1):
+        u[0] = zplane
+        u[65] = zplane
+
+    def zero_rows(x, _):
+        for h in range(2):
+            for u in (u0, u1):
+                u[x + 1, h, pl.ds(7, 1), :] = zrow
+                u[x + 1, h, pl.ds(72, 1), :] = zrow
+            for r in range(2):
+                hy[r, 0, x, h, pl.ds(1, 7), :] = jnp.zeros((7, 128), F32)
+                hy[r, 1, x, h, pl.ds(0, 7), :] = jnp.zeros((7, 128), F32)
+        return 0
+
+    lax.fori_loop(0, 64, zero_rows, 0, unroll=2)
+
+    def zero_halo(side):
         def body(x, _):
-            for h in range(2):
-                u0[x, h, pl.ds(row, 1), :] = zrow
-                u1[x, h, pl.ds(row, 1), :] = zrow
+            for r in range(2):
+                for h in range(2):
+                    hy[r, side, x, h, pl.ds(7 * side, 1), :] = zrow
             return 0
 
-        lax.fori_loop(1, 65, body, 0)
-
-    @pl.when(gy == 0)
-    def _():
-        zero_rows(7)
-
-    @pl.when(gy == ny - 1)
-    def _():
-        zero_rows(72)
-
-    @pl.when(gz == 0)
-    def _():
-        zr[0, 0] = jnp.zeros((64, 128), F32)
-        zr[1, 0] = jnp.zeros((64, 128), F32)
-
-    @pl.when(gz == nz - 1)
-    def _():
-        zr[0, 1] = jnp.zeros((64, 128), F32)
-        zr[1, 1] = jnp.zeros((64, 128), F32)
+        lax.fori_loop(0, 64, body, 0)
+
+    for side in range(2):
+        d = 2 * side - 1
+
+        @pl.when(jnp.logical_not(has("gy", d)))
+        def _():
+            zero_halo(side)
+
+        @pl.when(jnp.logical_not(has("gz", d)))
+        def _():
+            for r in range(2):
+                zr[r, side] = jnp.zeros((64, 128), F32)
 
     for p in (0, 1, 2, 67, 68, 69, 70):
         u2[p] = zplane
@@ -181,10 +180,10 @@
         xs = pl.ds(1, 64)
         every = slice(None)
         plan = [
-            ("gx", 1, u.at[(64,) + x_in], u.at[(0,) + x_in]),
-            ("gx", -1, u.at[(1,) + x_in], u.at[(65,) + x_in]),
-            ("gy", 1, u.at[xs, every, pl.ds(71, 1), every], u.at[xs, every, pl.ds(7, 1), every]),
-            ("gy", -1, u.at[xs, every, pl.ds(8, 1), every], u.at[xs, every, pl.ds(72, 1), every]),
+            ("gx", 1, u.at[(64,) + x_in], hx.at[r, 0]),
+            ("gx", -1, u.at[(1,) + x_in], hx.at[r, 1]),
+            ("gy", 1, u.at[xs, every, pl.ds(71, 1), every], hy.at[r, 0, every, every, pl.ds(0, 1), every]),
+            ("gy", -1, u.at[xs, every, pl.ds(8, 1), every], hy.at[r, 1, every, every, pl.ds(7, 1), every]),
             ("gz", 1, ez.at[r], zr.at[r, 0]),
             ("gz", -1, ez.at[r], zr.at[r, 1]),
         ]
@@ -218,43 +217,31 @@
     pl.semaphore_wait(barrier, count)
     start(round0[:4])
 
-    group8 = group[:8]
     first8, last8 = first[:8], last[:8]
 
-    def pack(n, packed):
-        for j in range(8):
-            x = 8 * n + j
-            both = jnp.where(first, u0[x + 1, 0, pl.ds(8, 64), :], u0[x + 1, 1, pl.ds(8, 64), :])
-            packed = jnp.where(group == x, pltpu.roll(both, 2 * x, 1), packed)
-        return packed
-
-    ez[0] = lax.fori_loop(0, 8, pack, jnp.zeros((64, 128), F32))
-    ez[1] = jnp.zeros((64, 128), F32)
+    def pack_faces(r, u):
+        def pack(n, packed):
+            for j in range(8):
+                x = 8 * n + j
+                both = jnp.where(first, u[x + 1, 0, pl.ds(8, 64), :], u[x + 1, 1, pl.ds(8, 64), :])
+                packed = jnp.where(group == x, pltpu.roll(both, 2 * x, 1), packed)
+            return packed
+
+        ez[r] = lax.fori_loop(0, 8, pack, jnp.zeros((64, 128), F32))
+
+    pack_faces(0, u0)
     start(round0[4:])
-
-    def beside_z(r, u, starts, x0, group_size):
-        halo = [zr[r, 0, pl.ds(y, 8), :] for y in starts]
+    first8, last8 = first[:8], last[:8]
+    zero8 = jnp.zeros((8, 128), F32)
+
+    def beside_z(u, starts, x0, group_size):
         for j in range(group_size):
-            x = x0 + j
-            shift = lax.rem(128 - 2 * x, 128)
             for k, y in enumerate(starts):
-                side = pltpu.roll(halo[k], shift, 1)
-                c = [u[x + 1, h, pl.ds(8 + y, 8), :] for h in range(2)]
+                c = [u[x0 + j + 1, h, pl.ds(8 + y, 8), :] for h in range(2)]
                 right = [pltpu.roll(c[h], 1, 1) for h in range(2)]
                 left = [pltpu.roll(c[h], 127, 1) for h in range(2)]
-                zs[j, k, 0] = jnp.where(first8, side, right[0]) + jnp.where(last8, left[1], left[0])
-                zs[j, k, 1] = jnp.where(first8, right[0], right[1]) + jnp.where(last8, side, left[1])
-
-    def pack_ends_of(v, starts, x0, group_size):
-        packed = [ez[1, pl.ds(y, 8), :] for y in starts]
-        for j in range(group_size):
-            x = x0 + j
-            here = group8 == x
-            for k, y in enumerate(starts):
-                both = jnp.where(first8, v[x + 1, 0, pl.ds(8 + y, 8), :], v[x + 1, 1, pl.ds(8 + y, 8), :])
-                packed[k] = jnp.where(here, pltpu.roll(both, 2 * x, 1), packed[k])
-        for k, y in enumerate(starts):
-            ez[1, pl.ds(y, 8), :] = packed[k]
+                zs[j, k, 0] = jnp.where(first8, zero8, right[0]) + jnp.where(last8, left[1], left[0])
+                zs[j, k, 1] = jnp.where(first8, right[0], right[1]) + jnp.where(last8, zero8, left[1])
 
     def relax(u, v, off, starts, x0, group_size):
         def planes(p):
@@ -271,40 +258,58 @@
                     v[x + off, h, pl.ds(8 + y, 8), :] = (total + zs[j, k, h]) * SEVENTH
             before, here = here, after
 
-    def pipelined(r, u, v, off, count, place, group_size):
-        beside_z(r, u, *place(0), group_size)
+    def sweep(u, v, off):
+        every = 64 // GI
+        count = (8 // NI) * every
+
+        def place(n):
+            y = 8 * NI * (n // every)
+            return [pl.multiple_of(y + 8 * k, 8) for k in range(NI)], GI * lax.rem(n, every)
+
+        beside_z(u, *place(0), GI)
 
         def body(n, _):
-            if r == 0:
-                pack_ends_of(v, *place(jnp.maximum(n - 1, 0)), group_size)
-            relax(u, v, off, *place(n), group_size)
-            beside_z(r, u, *place(jnp.minimum(n + 1, count - 1)), group_size)
+            relax(u, v, off, *place(n), GI)
+            beside_z(u, *place(jnp.minimum(n + 1, count - 1)), GI)
             return 0
 
         lax.fori_loop(0, count, body, 0)
-        if r == 0:
-            pack_ends_of(v, *place(count - 1), group_size)
-
-    def sweep(r, copies, u, v, off):
-        arrive(copies[4:])
+
+    def add_halos(r, copies, v, off):
+        arrive(copies)
         even = lax.rem(lane, 2) == 0
-        zr[r, 0] = jnp.where(even, pltpu.roll(zr[r, 0], 1, 1), pltpu.roll(zr[r, 1], 127, 1))
-        arrive(copies[:2])
-        every = 64 // GI
-
-        def inner(n):
-            y = 8 + 8 * NI * (n // every)
-            return [pl.multiple_of(y + 8 * k, 8) for k in range(NI)], GI * lax.rem(n, every)
-
-        pipelined(r, u, v, off, (6 // NI) * every, inner, GI)
-        arrive(copies[2:4])
-        pipelined(r, u, v, off, 64 // GO, lambda n: ([0, 56], GO * n), GO)
+        zr[r, 0] = jnp.where(even, pltpu.roll(zr[r, 0], 1, 1), pltpu.roll(zr[r, 1], 127, 1)) * SEVENTH
+        for side, p in enumerate((off, off + 63)):
+
+            @pl.when(has("gx", 2 * side - 1))
+            def _():
+                for h in range(2):
+                    v[p, h, pl.ds(8, 64), :] = v[p, h, pl.ds(8, 64), :] + hx[r, side, h] * SEVENTH
+
+        def body(n, _):
+            for j in range(GH):
+                x = GH * n + j
+                side = pltpu.roll(zr[r, 0], lax.rem(128 - 2 * x, 128), 1)
+                for h in range(2):
+                    for k in range(8):
+                        at_end = jnp.where(last8 if h else first8, side[8 * k : 8 * k + 8], zero8)
+                        if k in (0, 7):
+                            at_end = at_end + hy[r, k // 7, x, h] * SEVENTH
+                        rows = pl.ds(8 + 8 * k, 8)
+                        v[x + off, h, rows, :] = v[x + off, h, rows, :] + at_end
+            return 0
+
+        lax.fori_loop(0, 64 // GH, body, 0)
 
     loads[2].wait()
     loads[3].wait()
-    sweep(0, round0, u0, u1, 1)
-    start(round1)
-    sweep(1, round1, u1, u2, 3)
+    sweep(u0, u1, 1)
+    add_halos(0, round0, u1, 1)
+    start(round1[:4])
+    pack_faces(1, u1)
+    start(round1[4:])
+    sweep(u1, u2, 3)
+    add_halos(1, round1, u2, 3)
 
     topx = gx == nx - 1
 
@@ -562,7 +567,8 @@
         v((2, 4, 96, 128), F32), v((34, 40, 512), F32), v((512, 256), BF16), v((256, 256), BF16),
         v((40, 40, 128), F32), v((40, 40, 128), F32), v((2, 3, 40, 128), F32), v((2, 3, 40, 128), F32),
         v((3, 40, 128), F32), v((42, 2, 40, 128), F32), v((42, 2, 56, 128), F32), v((42, 2, 56, 128), F32),
-        v((max(GI, GO), max(NI, 2), 2, 8, 128), F32),
+        v((GI, NI, 2, 8, 128), F32),
+        v((2, 2, 2, 64, 128), F32), v((2, 2, 64, 2, 8, 128), F32),
     ]
     scratch += [v((SEND[dx][1], SEND[dy][1], 128), F32) for dx, dy in XY8]
     scratch += [v((2, TSEND[dx][1], SEND[dy][1], 128), F32) for dx, dy in XY8]

time: 42.9 us -> 37.7 us (0.88); the launches traced: 42.7 us -> 37 us
  Pallas kernels: 42.7 us -> 37 us
    pallas_call x1, Pallas kernels: 40.7 us -> 35 us  [on_device(): pl.pallas_call(kernel, out_shape=(v((71, 2, 80, 128), F32), v((33, 2, 40,...]
where the time goes in v3:
time: 37.7 us; the launch traced here: 37 us
  Pallas kernels  37 us (98%)
    pallas_call x1, Pallas kernels, on_device(): pl.pallas_call(kernel, out_shape=(v((71, 2, 80, 128), F32), v((33, 2, 40,...  35 us
    pallas_call x1, Pallas kernels, on_device(): pl.pallas_call(finish_kernel, out_shape=jax.ShapeDtypeStruct(start_field....  2.01 us

profile of v3, /device:TPU:10, one launch (start us, length us, event | category | flops | bytes accessed | tf_op | source)
XLA Modules:
  0.0 37.0 jit_solution(6958726175305997529)
XLA Ops:
  0.0 35.0 %shard_map.28 = (f32[71,2,80,128]{3,2,1,0:T(8,128)S(1)}, f32[33,2,40,128]{3,2,1,0:T(8,128)S(1)}) custom-call(f32[64,64,256]{2,1,0:T(8,128)} %s_in.1, f32[64,64,256]{2,1,0:T(8,128)} %b_in.1), custom_call_target="tpu_custom_call" | custom-call | tf_op jit(solution)/shard_map/pallas_call | solution.py:581
  35.0 2.0 %shard_map.29 = f32[64,64,256]{2,1,0:T(8,128)} custom-call(f32[71,2,80,128]{3,2,1,0:T(8,128)S(1)} %get-tuple-element.7.u2, f32[33,2,40,128]{3,2,1,0:T(8,128)S(1)} %get-tuple-element.8.fz), custom_call_target="tpu_custom_call" | custom-call | tf_op jit(solution)/shard_map/pallas_call | solution.py:590

commit v4 on v3

--- a/solution.py
+++ b/solution.py
@@ -12,7 +12,7 @@
 BF16 = jnp.bfloat16
 SEVENTH = 1.0 / 7.0
 UE, UA, UF = 8, 8, 2
-NI, GI, GH = 4, 8, 8
+NI, GI, GH = 4, 8, 32
 UC = (8, 6, 7)
 AXES = ("gx", "gy", "gz")
 SEND = {-1: (3, 4), 0: (3, 34), 1: (32, 5)}
@@ -336,7 +336,7 @@
 
     def restrict_half(n, _):
         i = 17 * n
-        lax.fori_loop(i, i + 17, restrict, 0)
+        lax.fori_loop(0, 18, lambda k, c: restrict(16 * n + k, c), 0, unroll=2)
         got = dot3(qb[pl.ds(i, 17)].reshape(680, 512), wr[...])
         main = got[:, :128].reshape(17, 40, 128)
         gm[pl.ds(i + 3, 17)] = main

time: 37.7 us -> 36.8 us (0.976)
  Pallas kernels: 37 us -> 36.1 us
    pallas_call x1, Pallas kernels: 35 us -> 34 us  [on_device(): pl.pallas_call(kernel, out_shape=(v((71, 2, 80, 128), F32), v((33, 2, 40,...]
where the time goes in v4:
time: 36.8 us; the launch traced here: 36.1 us
  Pallas kernels  36.1 us (98%)
    pallas_call x1, Pallas kernels, on_device(): pl.pallas_call(kernel, out_shape=(v((71, 2, 80, 128), F32), v((33, 2, 40,...  34 us
    pallas_call x1, Pallas kernels, on_device(): pl.pallas_call(finish_kernel, out_shape=jax.ShapeDtypeStruct(start_field....  2.01 us

profile of v4, /device:TPU:10, one launch (start us, length us, event | category | flops | bytes accessed | tf_op | source)
XLA Modules:
  0.0 36.1 jit_solution(4249504651412047380)
XLA Ops:
  0.0 34.0 %shard_map.28 = (f32[71,2,80,128]{3,2,1,0:T(8,128)S(1)}, f32[33,2,40,128]{3,2,1,0:T(8,128)S(1)}) custom-call(f32[64,64,256]{2,1,0:T(8,128)} %s_in.1, f32[64,64,256]{2,1,0:T(8,128)} %b_in.1), custom_call_target="tpu_custom_call" | custom-call | tf_op jit(solution)/shard_map/pallas_call | solution.py:581
  34.1 2.0 %shard_map.29 = f32[64,64,256]{2,1,0:T(8,128)} custom-call(f32[71,2,80,128]{3,2,1,0:T(8,128)S(1)} %get-tuple-element.7.u2, f32[33,2,40,128]{3,2,1,0:T(8,128)S(1)} %get-tuple-element.8.fz), custom_call_target="tpu_custom_call" | custom-call | tf_op jit(solution)/shard_map/pallas_call | solution.py:590

commit v5 on v4

--- a/solution.py
+++ b/solution.py
@@ -11,7 +11,7 @@
 F32 = jnp.float32
 BF16 = jnp.bfloat16
 SEVENTH = 1.0 / 7.0
-UE, UA, UF = 8, 8, 2
+UE, UA, UF = 8, 10, 2
 NI, GI, GH = 4, 8, 32
 UC = (8, 6, 7)
 AXES = ("gx", "gy", "gz")
@@ -221,13 +221,13 @@
 
     def pack_faces(r, u):
         def pack(n, packed):
-            for j in range(8):
-                x = 8 * n + j
+            for j in range(32):
+                x = 32 * n + j
                 both = jnp.where(first, u[x + 1, 0, pl.ds(8, 64), :], u[x + 1, 1, pl.ds(8, 64), :])
                 packed = jnp.where(group == x, pltpu.roll(both, 2 * x, 1), packed)
             return packed
 
-        ez[r] = lax.fori_loop(0, 8, pack, jnp.zeros((64, 128), F32))
+        ez[r] = lax.fori_loop(0, 2, pack, jnp.zeros((64, 128), F32))
 
     pack_faces(0, u0)
     start(round0[4:])

time: 36.8 us -> 36.3 us (0.986)
  Pallas kernels: 36.1 us -> 35.7 us
    pallas_call x1, Pallas kernels: 34 us -> 33.7 us  [on_device(): pl.pallas_call(kernel, out_shape=(v((71, 2, 80, 128), F32), v((33, 2, 40,...]
where the time goes in v5:
time: 36.3 us; the launch traced here: 35.7 us
  Pallas kernels  35.7 us (98%)
    pallas_call x1, Pallas kernels, on_device(): pl.pallas_call(kernel, out_shape=(v((71, 2, 80, 128), F32), v((33, 2, 40,...  33.7 us
    pallas_call x1, Pallas kernels, on_device(): pl.pallas_call(finish_kernel, out_shape=jax.ShapeDtypeStruct(start_field....  2.01 us

profile of v5, /device:TPU:10, one launch (start us, length us, event | category | flops | bytes accessed | tf_op | source)
XLA Modules:
  0.0 35.7 jit_solution(2462875724390221243)
XLA Ops:
  0.0 33.7 %shard_map.28 = (f32[71,2,80,128]{3,2,1,0:T(8,128)S(1)}, f32[33,2,40,128]{3,2,1,0:T(8,128)S(1)}) custom-call(f32[64,64,256]{2,1,0:T(8,128)} %s_in.1, f32[64,64,256]{2,1,0:T(8,128)} %b_in.1), custom_call_target="tpu_custom_call" | custom-call | tf_op jit(solution)/shard_map/pallas_call | solution.py:581
  33.7 2.0 %shard_map.29 = f32[64,64,256]{2,1,0:T(8,128)} custom-call(f32[71,2,80,128]{3,2,1,0:T(8,128)S(1)} %get-tuple-element.7.u2, f32[33,2,40,128]{3,2,1,0:T(8,128)S(1)} %get-tuple-element.8.fz), custom_call_target="tpu_custom_call" | custom-call | tf_op jit(solution)/shard_map/pallas_call | solution.py:590
